TPU v7x, 128 devices: a whole 4x4x4 slice. The times are simulated.
128 devices in a mesh: gz: 128 (over x, y, z, core).
Axes of the slice: x: 4, y: 4, z: 4, core: 2. Of those that a mesh axis runs over, the one named last changes fastest.
Arguments:
- density: float32 [2, 128, 256, 256], P(None, 'gz'), may hold values from 0.02 to 0.8
- kernel_hat: float32 [256, 512, 512], P(None, 'gz'), may hold values from 0.37 to 7, as said below
Outputs:
- potential: float32 [2, 128, 256, 256], P(None, 'gz')
- energies: float32 [2], replicated
Inputs may be any that keep to these rules, and one draw needn't show every extreme that they name: kernel_hat at (a, b, c) equals kernel_hat at ((-a) mod 256, (-b) mod 512, (-c) mod 512).
All inputs are finite; a program needn't handle non-finite values.
Results may differ from a plain program's by a relative error of at most 0.00015.
Values sent between devices are 32-bit elements; how exact they have to be, the bound alone decides.
No kernel may reach another device: no remote copies, remote signals or barrier semaphores. Data moves between devices by JAX's collectives and lax.ppermute only.
A program may use at most 64 MiB of HBM per device.

v0:
```python
import math

import jax
import jax.numpy as jnp
import numpy as np
from jax import lax
from jax.experimental import pallas as pl
from jax.experimental.pallas import tpu as pltpu
from jax.sharding import Mesh
from jax.sharding import PartitionSpec as P

GZ = ("gz_0", "gz_1", "gz_2", "gz_3")
HGRID = 0.35
STENCIL = (0.8, -0.2, 4.0 / 105.0, -1.0 / 280.0)
KAPPA = 0.804
MU_X = 0.2195149727645171
BETA_C = 0.06672455060314922
GAMMA_C = 0.031090690869654894
FZ_CURV = 1.709921
PARAMS_UNPOL = (0.031091, 0.2137, 7.5957, 3.5876, 1.6382, 0.49294)
PARAMS_POL = (0.015545, 0.20548, 14.1189, 6.1977, 3.3662, 0.62517)
PARAMS_STIFF = (0.016887, 0.11125, 10.357, 3.6231, 0.88026, 0.49671)

F32 = jnp.float32
BF16 = jnp.bfloat16
NZ, NY, NX = 128, 256, 256
MZ, MY, MX = 256, 512, 512
ND = 128
A_ROWS = 16
B_ROWS = 10
D_ROWS = 12
CELLS = NZ * NY * NX
VMEM = pl.BlockSpec(memory_space=pltpu.VMEM)
SMEM = pl.BlockSpec(memory_space=pltpu.SMEM)


def slope_matrix(n):
    m = np.zeros((n, n))
    for k, c in enumerate(STENCIL, 1):
        m += np.diag(np.full(n - k, c / HGRID), k) - np.diag(np.full(n - k, c / HGRID), -k)
    return m.astype(np.float32)


def halves(m):
    m = np.asarray(m, np.float32)
    hi = m.astype(BF16)
    lo = (m - hi.astype(np.float32)).astype(BF16)
    return np.stack([hi, lo])


def owned_frequencies():
    q = np.arange(ND)
    first = np.where(q < ND // 2, 4 * q + 1, 4 * q)
    return first, first + 1


def y_forward():
    y = np.arange(NY)
    rows = []
    for ky in owned_frequencies():
        angle = 2.0 * np.pi * (np.outer(ky, y) % MY) / MY
        rows += [np.cos(angle), -np.sin(angle)]
    return halves(np.concatenate(rows, 0))


def y_backward():
    y = np.arange(NY)
    cols = []
    for ky in owned_frequencies():
        angle = 2.0 * np.pi * (np.outer(y, ky) % MY) / MY
        weight = np.where(ky == MY // 2, 1.0, 2.0) / (MX * MY * MZ)
        cols += [np.cos(angle) * weight, -np.sin(angle) * weight]
    return halves(np.concatenate(cols, 1))


def parity_matrix():
    m = np.zeros((NX, NX), np.float32)
    x = np.arange(NX)
    m[x, (x % 2) * (NX // 2) + x // 2] = 1.0
    return m


def rotation(angle):
    c, s = np.cos(angle), np.sin(angle)
    return np.block([[c, s], [-s, c]])


def x_forward():
    out = []
    k = np.arange(MX // 2)
    for parity in (0, 1):
        x = 2 * np.arange(NX // 2) + parity
        out.append(rotation(2.0 * np.pi * (np.outer(k, x) % MX) / MX).T)
    return np.stack([halves(m) for m in out])


def x_backward():
    out = []
    k = np.arange(MX // 2)
    for parity in (0, 1):
        x = 2 * np.arange(NX // 2) + parity
        out.append(rotation(2.0 * np.pi * (np.outer(k, x) % MX) / MX))
    return np.stack([halves(m) for m in out])


Z_CHUNK = 32


def z_forward():
    z = np.arange(NZ)
    rows = []
    for c in range(0, NZ, Z_CHUNK):
        low = np.arange(c, c + Z_CHUNK)
        kz = np.concatenate([low, low + NZ])
        rows.append(rotation(2.0 * np.pi * (np.outer(kz, z) % MZ) / MZ))
    return halves(np.concatenate(rows, 0))


def z_backward():
    out = []
    k = np.arange(NZ)
    for parity in (0, 1):
        z = 2 * np.arange(NZ // 2) + parity
        out.append(rotation(2.0 * np.pi * (np.outer(k, z) % MZ) / MZ).T)
    return np.stack([halves(m) for m in out])


def split(value):
    hi = value.astype(BF16)
    lo = (value - hi.astype(F32)).astype(BF16)
    return hi, lo


def dot1(a, b):
    return jnp.dot(a, b, preferred_element_type=F32)


def dot3(a_hi, a_lo, b_hi, b_lo):
    return dot1(a_hi, b_hi) + (dot1(a_lo, b_hi) + dot1(a_hi, b_lo))


def dot_exact(a, b):
    return jnp.dot(a, b, precision=lax.Precision.HIGHEST, preferred_element_type=F32)


def put_rows(ref, row, rows, value, count=ND, scale=1):
    for half in range(value.shape[1] // 128):
        ref[pl.ds(row + half, count, stride=rows * scale), :] = value[
            :, half * 128 : half * 128 + 128
        ]


def get_rows(ref, row, rows):
    return jnp.concatenate(
        [ref[pl.ds(row + half, ND, stride=rows), :] for half in range(2)], axis=1
    )


def gradient_kernel(dens_ref, slope_ref, out_ref):
    for spin in range(2):
        field = dens_ref[spin * NY : (spin + 1) * NY, :]
        grad = dot_exact(slope_ref[...], field)
        for part in range(2):
            rows = slice(part * 128, part * 128 + 128)
            put_rows(out_ref, spin * 4 + part * 2, A_ROWS, field[rows])
            put_rows(out_ref, 8 + spin * 4 + part * 2, A_ROWS, grad[rows])


def y_forward_kernel(dens_ref, parity_ref, table_ref, out_ref):
    hi, lo = split(dens_ref[0:NY, :] + dens_ref[NY : 2 * NY, :])
    parity = parity_ref[...]
    hi, lo = dot1(hi, parity), dot1(lo, parity)
    mean_row = jnp.sum(hi + lo, axis=0, keepdims=True)
    put_rows(out_ref, 8, B_ROWS, jnp.broadcast_to(mean_row, (ND, NX)))
    hi, lo = hi.astype(BF16), lo.astype(BF16)
    for s in range(4):
        rows = slice(s * ND, (s + 1) * ND)
        value = dot3(table_ref[0, rows, :], table_ref[1, rows, :], hi, lo)
        put_rows(out_ref, s * 2, B_ROWS, value)


def pw_piece(root, params):
    radius = root * root
    scale = 2.0 * params[0]
    series = root * (
        scale * params[2]
        + root * (scale * params[3] + root * (scale * params[4] + root * (scale * params[5])))
    )
    slope = root * (
        0.5 * scale * params[2]
        + root
        * (
            scale * params[3]
            + root * (1.5 * scale * params[4] + root * (2.0 * scale * params[5]))
        )
    )
    inv = 1.0 / (series * (series + 1.0))
    logarithm = jnp.log(1.0 + inv * (series + 1.0))
    front = -scale - (scale * params[1]) * radius
    value = front * logarithm
    deriv = (-scale * params[1]) * radius * logarithm - front * slope * inv
    return value, deriv


def exchange_piece(dens, inv_root, sigma):
    root = 2.0 * dens * inv_root * inv_root
    inv2 = inv_root * inv_root
    inv4 = inv2 * inv2
    reduced = sigma * (inv4 * inv4) * (1.0 / (3.0 * math.pi**2) ** (2.0 / 3.0))
    damp = 1.0 / (1.0 + (MU_X / KAPPA) * reduced)
    enhance = (1.0 + KAPPA) - KAPPA * damp
    front = -0.75 * (3.0 / math.pi) ** (1.0 / 3.0)
    damp_sq = MU_X * damp * damp
    energy = front * dens * root * enhance
    d_dens = (4.0 / 3.0 * front) * root * (enhance - 2.0 * reduced * damp_sq)
    d_sigma = (0.5 * front / (3.0 * math.pi**2) ** (2.0 / 3.0)) * damp_sq * inv4
    return energy, d_dens, d_sigma, root


def xc_point(up, down, sigma_uu, sigma_ud, sigma_dd):
    inv_up = jnp.exp(jnp.log(2.0 * up) * (-1.0 / 3.0))
    inv_down = jnp.exp(jnp.log(2.0 * down) * (-1.0 / 3.0))
    e_up, d_up, d_uu, root_up = exchange_piece(up, inv_up, sigma_uu)
    e_down, d_down, d_dd, root_down = exchange_piece(down, inv_down, sigma_dd)
    dens = up + down
    sixth = jnp.exp(jnp.log(dens) * (-1.0 / 6.0))
    inv_third = sixth * sixth
    third = dens * inv_third * inv_third
    inv_dens = inv_third * inv_third * inv_third
    zeta = (up - down) * inv_dens
    plus = 2.0 * up * inv_dens
    minus = 2.0 * down * inv_dens
    plus_cube = root_up * inv_third
    minus_cube = root_down * inv_third
    f_scale = 1.0 / (2.0 ** (4.0 / 3.0) - 2.0)
    f = (plus * plus_cube + minus * minus_cube - 2.0) * f_scale
    f_slope = (plus_cube - minus_cube) * (4.0 / 3.0 * f_scale)
    root = (3.0 / (4.0 * math.pi)) ** (1.0 / 6.0) * sixth
    e0, e0_d = pw_piece(root, PARAMS_UNPOL)
    e1, e1_d = pw_piece(root, PARAMS_POL)
    ac, ac_d = pw_piece(root, PARAMS_STIFF)
    z2 = zeta * zeta
    z3_4 = 4.0 * z2 * zeta
    z4 = z2 * z2
    one_z4 = (1.0 - z4) * (-1.0 / FZ_CURV)
    f_z4 = f * z4
    f_one = f * one_z4
    diff = e1 - e0
    local = e0 + ac * f_one + diff * f_z4
    local_r = e0_d + ac_d * f_one + (e1_d - e0_d) * f_z4
    fz3 = z3_4 * f
    local_z = ac * (f_slope * one_z4 + (1.0 / FZ_CURV) * fz3) + diff * (f_slope * z4 + fz3)
    phi = 0.5 * (plus_cube * plus_cube + minus_cube * minus_cube)
    inv_phi = 1.0 / phi
    phi_log_slope = (third * (1.0 / 3.0)) * (inv_up - inv_down) * inv_phi
    g3 = GAMMA_C * phi * phi * phi
    inv_g3 = (1.0 / GAMMA_C) * inv_phi * inv_phi * inv_phi
    grow = jnp.exp(-local * inv_g3)
    weight_a = (BETA_C / GAMMA_C) / (grow - 1.0)
    sigma = sigma_uu + 2.0 * sigma_ud + sigma_dd
    ct = math.pi / (16.0 * (3.0 * math.pi**2) ** (1.0 / 3.0))
    kt = ct * inv_third * inv_dens * inv_dens * inv_phi * inv_phi
    t2 = sigma * kt
    w = weight_a * t2
    num = 1.0 + w
    den = num + w * w
    add = (BETA_C / GAMMA_C) * t2 * num
    both = den + add
    inv_both = 1.0 / (den * both)
    h = g3 * jnp.log(1.0 + add * (inv_both * both))
    h_t = (BETA_C / GAMMA_C) * g3 * (1.0 + 2.0 * w) * inv_both
    h_a = -(w * w * w) * (2.0 + w) * grow * inv_both
    total = local + h
    ht_t2 = h_t * t2
    one_ha = 1.0 + h_a
    d_n = total - (1.0 / 3.0) * one_ha * local_r - (7.0 / 3.0) * ht_t2
    d_z = one_ha * local_z + phi_log_slope * (3.0 * (h - h_a * local) - 2.0 * ht_t2)
    d_sigma = dens * h_t * kt
    energy = e_up + e_down + dens * total
    return (
        energy,
        d_up + d_n + minus * d_z,
        d_down + d_n - plus * d_z,
        d_uu + d_sigma,
        2.0 * d_sigma,
        d_dd + d_sigma,
    )


def xc_kernel(in_ref, slope_z_ref, slope_x_ref, out_ref, energy_ref, dens, gz, gy, gx):
    for spin in range(2):
        for part in range(2):
            rows = slice(part * 128, part * 128 + 128)
            field = get_rows(in_ref, spin * 4 + part * 2, A_ROWS)
            dens[spin, rows, :] = field
            gy[spin, rows, :] = get_rows(in_ref, 8 + spin * 4 + part * 2, A_ROWS)
            gz[spin, rows, :] = dot_exact(slope_z_ref[...], field)
        gx[spin] = dot_exact(dens[spin], slope_x_ref[...])

    def chunk(i, total):
        rows = pl.ds(pl.multiple_of(i * 8, 8), 8)
        zu, zd = gz[0, rows, :], gz[1, rows, :]
        yu, yd = gy[0, rows, :], gy[1, rows, :]
        xu, xd = gx[0, rows, :], gx[1, rows, :]
        energy, d_up, d_down, d_uu, d_ud, d_dd = xc_point(
            dens[0, rows, :],
            dens[1, rows, :],
            zu * zu + yu * yu + xu * xu,
            zu * zd + yu * yd + xu * xd,
            zd * zd + yd * yd + xd * xd,
        )
        dens[0, rows, :] = d_up
        dens[1, rows, :] = d_down
        for ref, gu, gd in ((gz, zu, zd), (gy, yu, yd), (gx, xu, xd)):
            ref[0, rows, :] = 2.0 * d_uu * gu + d_ud * gd
            ref[1, rows, :] = 2.0 * d_dd * gd + d_ud * gu
        return total + energy

    total = lax.fori_loop(0, 32, chunk, jnp.zeros((8, NX), F32))
    energy_ref[0, 0] = jnp.sum(total)
    for spin in range(2):
        div_x = dot_exact(gx[spin], slope_x_ref[...])
        for part in range(2):
            rows = slice(part * 128, part * 128 + 128)
            div_z = dot_exact(slope_z_ref[...], gz[spin, rows, :])
            put_rows(
                out_ref, spin * 4 + part * 2, A_ROWS, dens[spin, rows, :] - (div_z + div_x[rows])
            )
            put_rows(out_ref, 8 + spin * 4 + part * 2, A_ROWS, gy[spin, rows, :])


def hartree_kernel(
    in_ref, filt_ref, weight_ref, exc_ref, wx_ref, wz_ref, wzi_ref, wxi_ref, out_ref,
    xp, sums, back,
):
    even = [in_ref[pl.ds(r, ND, stride=B_ROWS), :] for r in range(0, B_ROWS, 2)]
    odd = [in_ref[pl.ds(r, ND, stride=B_ROWS), :] for r in range(1, B_ROWS, 2)]
    zero = jnp.zeros((ND, 128), F32)
    even.append(zero)
    odd.append(zero)
    for slot in range(3):
        parts = []
        for parity, source in ((0, even), (1, odd)):
            hi, lo = split(jnp.concatenate(source[2 * slot : 2 * slot + 2], axis=1))
            parts.append(dot3(hi, lo, wx_ref[parity, 0], wx_ref[parity, 1]))
        for half, value in ((0, parts[0] + parts[1]), (1, parts[0] - parts[1])):
            cols = slice(half * 256, half * 256 + 256)
            hi, lo = split(value)
            xp[slot, 0, 0:128, cols] = hi[:, 0:256]
            xp[slot, 0, 128:256, cols] = hi[:, 256:512]
            xp[slot, 1, 0:128, cols] = lo[:, 0:256]
            xp[slot, 1, 128:256, cols] = lo[:, 256:512]
    energy = jnp.zeros((8, MX), F32)
    for slot in range(3):
        weight = weight_ref[slot]

        def chunk(c, acc, slot=slot):
            rows = pl.ds(pl.multiple_of(c * 128, 128), 128)
            spec = dot3(wz_ref[0, rows, :], wz_ref[1, rows, :], xp[slot, 0], xp[slot, 1])
            low = pl.ds(pl.multiple_of(c * Z_CHUNK, Z_CHUNK), Z_CHUNK)
            high = pl.ds(pl.multiple_of(NZ + c * Z_CHUNK, Z_CHUNK), Z_CHUNK)
            f_low, f_high = filt_ref[slot, low, :], filt_ref[slot, high, :]
            for kind in range(2):
                a = spec[kind * 64 : kind * 64 + 32]
                b = spec[kind * 64 + 32 : kind * 64 + 64]
                fa, fb = a * f_low, b * f_high
                power = a * fa + b * fb
                acc = acc + (power[0:8] + power[8:16] + power[16:24] + power[24:32])
                dest = pl.ds(pl.multiple_of(kind * NZ + c * Z_CHUNK, Z_CHUNK), Z_CHUNK)
                for parity, value in ((0, fa + fb), (1, fa - fb)):
                    hi, lo = split(value)
                    sums[parity, 0, dest, :] = hi
                    sums[parity, 1, dest, :] = lo
            return acc

        acc = lax.fori_loop(0, NZ // Z_CHUNK, chunk, jnp.zeros((8, MX), F32))
        energy = energy + weight * acc
        for parity in range(2):
            grid = dot3(
                wzi_ref[parity, 0], wzi_ref[parity, 1], sums[parity, 0], sums[parity, 1]
            )
            for sign in range(2):
                a, b = grid[:, 0:256], grid[:, 256:512]
                hi, lo = split(a + b if sign == 0 else a - b)
                for part, value in ((0, hi), (1, lo)):
                    rows = slice(parity * 64, parity * 64 + 64)
                    back[sign, part, rows, 0:256] = value[0:64]
                    back[sign, part, rows, 256:512] = value[64:128]
        for sign in range(2):
            value = dot3(back[sign, 0], back[sign, 1], wxi_ref[sign, 0], wxi_ref[sign, 1])
            for parity in range(2):
                for kind in range(2 if slot < 2 else 1):
                    put_rows(
                        out_ref,
                        parity * D_ROWS + slot * 4 + kind * 2 + sign,
                        D_ROWS,
                        value[parity * 64 : parity * 64 + 64, kind * 128 : kind * 128 + 128],
                        count=64,
                        scale=2,
                    )
    put_rows(out_ref, 10, D_ROWS, jnp.full((ND, 128), exc_ref[0, 0], F32))
    put_rows(out_ref, 11, D_ROWS, jnp.full((ND, 128), jnp.sum(energy), F32))


def divergence_kernel(in_ref, slope_ref, out_ref):
    for spin in range(2):
        flux = jnp.concatenate(
            [get_rows(in_ref, 8 + spin * 4 + part * 2, A_ROWS) for part in range(2)], axis=0
        )
        rest = jnp.concatenate(
            [get_rows(in_ref, spin * 4 + part * 2, A_ROWS) for part in range(2)], axis=0
        )
        out_ref[spin * NY : (spin + 1) * NY, :] = rest - dot_exact(slope_ref[...], flux)


def potential_kernel(in_ref, v_ref, table_ref, parity_ref, out_ref, energy_ref):
    field = jnp.concatenate([get_rows(in_ref, 2 * s, D_ROWS) for s in range(4)], axis=0)
    hi, lo = split(field)
    grid = dot3(table_ref[0], table_ref[1], hi, lo)
    mean_row = jnp.concatenate([in_ref[8:9, :], in_ref[9:10, :]], axis=1)
    grid = grid + mean_row * (1.0 / (MX * MY * MZ))
    hi, lo = split(grid)
    hartree = dot1(hi, parity_ref[...]) + dot1(lo, parity_ref[...])
    for spin in range(2):
        rows = slice(spin * NY, (spin + 1) * NY)
        out_ref[rows, :] = v_ref[rows, :] + hartree
    exc = jnp.sum(in_ref[pl.ds(10, ND, stride=D_ROWS), :], axis=0, keepdims=True)
    power = jnp.sum(in_ref[pl.ds(11, ND, stride=D_ROWS), :], axis=0, keepdims=True)
    energy_ref[0] = jnp.sum(exc) * (1.0 / (128.0 * CELLS))
    energy_ref[1] = jnp.sum(power) * (0.5 / (128.0 * CELLS * MX * MY * MZ))


def call(kernel, outs, n_in, flops, scratch=(), smem_in=(), smem_out=(), limit=48):
    single = not isinstance(outs, (list, tuple))
    shapes = [outs] if single else list(outs)
    specs = [SMEM if i in smem_out else VMEM for i in range(len(shapes))]
    return pl.pallas_call(
        kernel,
        out_shape=shapes[0] if single else shapes,
        in_specs=[SMEM if i in smem_in else VMEM for i in range(n_in)],
        out_specs=specs[0] if single else specs,
        scratch_shapes=list(scratch),
        cost_estimate=pl.CostEstimate(flops=flops, bytes_accessed=4 << 20, transcendentals=0),
        compiler_params=pltpu.CompilerParams(vmem_limit_bytes=limit << 20),
        name=kernel.__name__,
    )


def arr(*shape):
    return jax.ShapeDtypeStruct(shape, F32)


def exchange(value, rows, group):
    shaped = value.reshape(ND * rows // group, group, 128)
    out = lax.all_to_all(shaped, GZ, split_axis=0, concat_axis=0, tiled=True)
    return out.reshape(ND * rows, 128)


def per_device(density, kernel_hat):
    q = lax.axis_index(GZ)
    dens = density.reshape(2 * NY, NX)
    slope_y = jnp.asarray(slope_matrix(NY))
    slope_z = jnp.asarray(slope_matrix(NZ))
    slope_x = jnp.asarray(slope_matrix(NX).T.copy())
    parity = parity_matrix()

    a_out = call(gradient_kernel, arr(ND * A_ROWS, 128), 2, 400_000_000)(dens, slope_y)
    a_in = exchange(a_out, A_ROWS, 8)
    b_out = call(y_forward_kernel, arr(ND * B_ROWS, 128), 3, 300_000_000)(
        dens, jnp.asarray(parity.astype(BF16)), jnp.asarray(y_forward())
    )
    b_in = exchange(b_out, B_ROWS, 2)
    start = jnp.where(q < ND // 2, 1, 0)
    picked = lax.dynamic_slice_in_dim(kernel_hat, start, 2, axis=1)
    filt = jnp.stack([picked[:, 0], picked[:, 1], kernel_hat[:, 0]])
    weights = jnp.stack(
        [
            jnp.where(q == ND // 2, 1.0, 2.0),
            jnp.full((), 2.0),
            jnp.where(q == 0, 1.0, 0.0),
        ]
    ).astype(F32)
    field = pltpu.VMEM((2, NY, NX), F32)
    c_out, exc = call(
        xc_kernel,
        [arr(ND * A_ROWS, 128), arr(1, 1)],
        3,
        4_000_000_000,
        scratch=[field] * 4,
        smem_out=(1,),
    )(a_in, slope_z, slope_x)
    c_in = exchange(c_out, A_ROWS, 8)
    d_out = call(
        hartree_kernel,
        arr(ND * D_ROWS, 128),
        8,
        4_000_000_000,
        scratch=[
            pltpu.VMEM((3, 2, 256, 512), BF16),
            pltpu.VMEM((2, 2, 256, 512), BF16),
            pltpu.VMEM((2, 2, 128, 512), BF16),
        ],
        smem_in=(2, 3),
    )(
        b_in,
        filt,
        weights,
        exc,
        jnp.asarray(x_forward()),
        jnp.asarray(z_forward()),
        jnp.asarray(z_backward()),
        jnp.asarray(x_backward()),
    )
    d_in = exchange(d_out, D_ROWS, 4)
    v = call(divergence_kernel, arr(2 * NY, NX), 2, 500_000_000)(c_in, slope_y)
    potential, energies = call(
        potential_kernel, [arr(2 * NY, NX), arr(2)], 4, 500_000_000, smem_out=(1,)
    )(d_in, v, jnp.asarray(y_backward()), jnp.asarray(parity.T.astype(BF16)))
    return potential.reshape(2, 1, NY, NX), energies


def solution(mesh):
    torus = Mesh(mesh.devices.reshape(4, 4, 4, 2), GZ)
    placed = (P(None, GZ, None, None), P(None, GZ, None))
    return jax.shard_map(
        per_device,
        mesh=torus,
        in_specs=placed,
        out_specs=(P(None, GZ, None, None), P()),
        check_vma=False,
    )
```

profile of v0, /device:TPU:1, one launch (start us, length us, event | category | flops | bytes accessed | tf_op | source)
XLA Modules:
  0.0 104.4 jit_solution(5042780005296953873)
XLA Ops:
  0.6 0.0 copy-start
  0.6 1.0 copy-done
  1.7 0.0 copy-start.4
  1.7 0.9 copy-done.4
  2.6 0.0 copy-start.1
  2.6 0.0 copy-start.2
  2.6 0.0 copy-start.6
  2.6 1.9 %gradient_kernel.1 = f32[2048,128]{1,0:T(8,128)} custom-call(f32[512,256]{1,0:T(8,128)S(1)} %bitcast.22, f32[256,256]{1,0:T(8,128)S(1)} %copy-done.4), custom_call_target="tpu_custom_call" | custom-call | flops 400000000 | bytes 4194304 | tf_op jit(solution)/shard_map/gradient_kernel/pallas_call | solution.py:467
  4.5 11.5 %all-to-all-start.1 = ((f32[256,8,128]{2,1,0:T(8,128)}), f32[256,8,128]{2,1,0:T(8,128)S(1)}, u32[]{:S(2)}, u32[]{:S(2)}) async-start(f32[256,8,128]{2,1,0:T(8,128)} %bitcast.8), calls=%async_computation.1 | async-start | bytes 2097152 | tf_op jit(solution)/shard_map/all_to_all | solution.py:455
  16.0 0.0 copy-done.1
  16.0 0.0 copy-done.2
  16.0 0.0 copy-done.6
  16.0 0.0 copy-start.12
  16.1 0.0 copy-start.13
  16.1 1.4 %y_forward_kernel.1 = f32[1280,128]{1,0:T(8,128)} custom-call(f32[512,256]{1,0:T(8,128)S(1)} %bitcast.23, bf16[256,256]{1,0:T(8,128)(2,1)S(1)} %copy-done.6, bf16[2,512,256]{2,1,0:T(8,128)(2,1)S(1)} %copy-done.2), custom_call_target="tpu_custom_call" | custom-call | flops 300000000 | bytes 4194304 | tf_op jit(solution)/shard_map/y_forward_kernel/pallas_call | solution.py:469
  17.5 17.7 %all-to-all-done.1 = f32[256,8,128]{2,1,0:T(8,128)S(1)} async-done(((f32[256,8,128]{2,1,0:T(8,128)}), f32[256,8,128]{2,1,0:T(8,128)S(1)}, u32[]{:S(2)}, u32[]{:S(2)}) %all-to-all-start.1) | async-done | bytes 1048608 | tf_op jit(solution)/shard_map/all_to_all | solution.py:455
  35.2 4.6 %all-to-all-start = ((f32[640,2,128]{2,1,0:T(2,128)}), f32[640,2,128]{2,1,0:T(2,128)S(1)}, u32[]{:S(2)}, u32[]{:S(2)}) async-start(f32[640,2,128]{2,1,0:T(2,128)} %bitcast.1), calls=%async_computation | async-start | bytes 1310720 | tf_op jit(solution)/shard_map/all_to_all | solution.py:455
  39.9 0.0 copy-done.12
  39.9 0.0 copy-done.13
  39.9 7.6 %xc_kernel.1 = (f32[2048,128]{1,0:T(8,128)}, f32[1,1]{1,0:T(1,128)}) custom-call(f32[2048,128]{1,0:T(8,128)S(1)} %bitcast.24, f32[128,128]{1,0:T(8,128)S(1)} %copy-done.13, f32[256,256]{1,0:T(8,128)S(1)} %copy-done.12), custom_call_target="tpu_custom_call" | custom-call | flops 4000000000 | bytes 4194304 | tf_op jit(solution)/shard_map/xc_kernel/pallas_call | solution.py:484
  47.4 7.5 %all-to-all-done = f32[640,2,128]{2,1,0:T(2,128)S(1)} async-done(((f32[640,2,128]{2,1,0:T(2,128)}), f32[640,2,128]{2,1,0:T(2,128)S(1)}, u32[]{:S(2)}, u32[]{:S(2)}) %all-to-all-start) | async-done | bytes 655392 | tf_op jit(solution)/shard_map/all_to_all | solution.py:455
  55.0 4.6 %all-to-all-start.3 = ((f32[256,8,128]{2,1,0:T(8,128)}), f32[256,8,128]{2,1,0:T(8,128)S(1)}, u32[]{:S(2)}, u32[]{:S(2)}) async-start(f32[256,8,128]{2,1,0:T(8,128)} %bitcast.12), calls=%async_computation.3 | async-start | bytes 2097152 | tf_op jit(solution)/shard_map/all_to_all | solution.py:455
  59.6 5.0 %constant_dynamic-slice_fusion = (f32[256,1,512]{2,1,0:T(1,128)S(1)}, f32[256,1,512]{2,1,0:T(1,128)S(1)}, f32[256,1,512]{2,1,0:T(1,128)}) fusion(f32[256,4,512]{2,1,0:T(4,128)} %param.14, s32[]{:T(128)S(6)} %select_n.12, s32[]{:T(128)S(6)} %add.13), kind=kLoop, calls=%fused_computation.5 | loop fusion | bytes 3145736 | tf_op jit(solution)/shard_map/slice | solution.py:475
  64.7 0.1 pad_maximum_fusion.1.weight_ref
  64.8 1.1 %copy_bitcast_fusion = (f32[1,256,512]{2,1,0:T(8,128)S(1)}, f32[1,256,512]{2,1,0:T(8,128)S(1)}) fusion(f32[256,1,512]{2,1,0:T(1,128)} %get-tuple-element.14, f32[256,1,512]{2,1,0:T(1,128)S(1)} %get-tuple-element.13), kind=kLoop, calls=%fused_computation.1 | loop fusion | bytes 2097152 | tf_op jit(solution)/shard_map/stack;squeeze | solution.py:475
  65.9 0.0 copy-start.8
  65.9 0.0 copy-start.9
  65.9 0.0 copy-start.10
  65.9 0.0 copy-start.11
  65.9 0.1 pad_maximum_fusion.filt_ref
  66.1 1.0 %copy-done.8 = bf16[2,2,256,512]{3,2,1,0:T(8,128)(2,1)S(1)} copy-done((bf16[2,2,256,512]{3,2,1,0:T(8,128)(2,1)S(1)}, bf16[2,2,256,512]{3,2,1,0:T(8,128)(2,1)}, u32[]{:S(2)}) %copy-start.8) | copy-done | bytes 1048600
  67.1 0.3 copy-done.9
  67.4 0.1 copy-done.10
  67.6 0.1 copy-done.11
  67.6 9.0 %hartree_kernel.1 = f32[1536,128]{1,0:T(8,128)} custom-call(f32[1280,128]{1,0:T(8,128)S(1)} %bitcast.26, f32[3,256,512]{2,1,0:T(8,128)S(1)} %pad_maximum_fusion.filt_ref, f32[3]{0:T(128)S(1)} %pad_maximum_fusion.1.weight_ref, f32[1,1]{1,0:T(1,128)} %get-tuple-element.6.exc_ref, bf16[2,2,256,512]{3,2,1,0:T(8,128)(2,1)S(1)} %copy-done.8, ...), custom_call_target="tpu_custom_call" | custom-call | flops 4000000000 | bytes 4194304 | tf_op jit(solution)/shard_map/hartree_kernel/pallas_call | solution.py:493
  76.6 0.0 copy-start.5
  76.6 2.3 %all-to-all-done.3 = f32[256,8,128]{2,1,0:T(8,128)S(1)} async-done(((f32[256,8,128]{2,1,0:T(8,128)}), f32[256,8,128]{2,1,0:T(8,128)S(1)}, u32[]{:S(2)}, u32[]{:S(2)}) %all-to-all-start.3) | async-done | bytes 1048608 | tf_op jit(solution)/shard_map/all_to_all | solution.py:455
  79.0 0.0 copy-start.3
  79.0 0.0 copy-start.7
  79.0 7.6 %all-to-all-start.2 = ((f32[384,4,128]{2,1,0:T(4,128)}), f32[384,4,128]{2,1,0:T(4,128)S(1)}, u32[]{:S(2)}, u32[]{:S(2)}) async-start(f32[384,4,128]{2,1,0:T(4,128)} %bitcast.10), calls=%async_computation.2 | async-start | bytes 1572864 | tf_op jit(solution)/shard_map/all_to_all | solution.py:455
  86.5 0.0 copy-done.5
  86.5 0.8 divergence_kernel.1.v_ref
  87.4 15.5 %all-to-all-done.2 = f32[384,4,128]{2,1,0:T(4,128)S(1)} async-done(((f32[384,4,128]{2,1,0:T(4,128)}), f32[384,4,128]{2,1,0:T(4,128)S(1)}, u32[]{:S(2)}, u32[]{:S(2)}) %all-to-all-start.2) | async-done | bytes 786464 | tf_op jit(solution)/shard_map/all_to_all | solution.py:455
  102.9 0.0 copy-done.3
  102.9 0.0 copy-done.7
  102.9 1.4 %potential_kernel.1 = (f32[512,256]{1,0:T(8,128)}, f32[2]{0:T(128)}) custom-call(f32[1536,128]{1,0:T(8,128)S(1)} %bitcast.21, f32[512,256]{1,0:T(8,128)S(1)} %divergence_kernel.1.v_ref, bf16[2,256,512]{2,1,0:T(8,128)(2,1)S(1)} %copy-done.3, bf16[256,256]{1,0:T(8,128)(2,1)S(1)} %copy-done.7), custom_call_target="tpu_custom_call" | custom-call | flops 500000000 | bytes 4194304 | tf_op jit(solution)/shard_map/potential_kernel/pallas_call | solution.py:516
  (1 shorter events, 0.0 us)
Async XLA Ops:
  0.6 1.0 copy-start
  1.7 0.9 copy-start.4
  2.6 13.4 %copy-start.1 = (f32[2,1,256,256]{3,2,1,0:T(8,128)S(1)}, f32[2,1,256,256]{3,2,1,0:T(8,128)}, u32[]{:S(2)}) copy-start(f32[2,1,256,256]{3,2,1,0:T(8,128)} %param.13) | copy-start | bytes 1572868
  2.6 13.4 %copy-start.2 = (bf16[2,512,256]{2,1,0:T(8,128)(2,1)S(1)}, bf16[2,512,256]{2,1,0:T(8,128)(2,1)}, u32[]{:S(2)}) copy-start(bf16[2,512,256]{2,1,0:T(8,128)(2,1)} %constant.63.clone.table_ref) | copy-start | bytes 1572868
  2.6 13.4 %copy-start.6 = (bf16[256,256]{1,0:T(8,128)(2,1)S(1)}, bf16[256,256]{1,0:T(8,128)(2,1)}, u32[]{:S(2)}) copy-start(bf16[256,256]{1,0:T(8,128)(2,1)} %constant.62.clone.parity_ref) | copy-start | bytes 393220
  4.5 30.7 %all-to-all-start.1 = ((f32[256,8,128]{2,1,0:T(8,128)}), f32[256,8,128]{2,1,0:T(8,128)S(1)}, u32[]{:S(2)}, u32[]{:S(2)}) async-start(f32[256,8,128]{2,1,0:T(8,128)} %bitcast.8), calls=%async_computation.1 | async-start | bytes 2097152 | tf_op jit(solution)/shard_map/all_to_all | solution.py:455
  16.0 23.8 %copy-start.12 = (f32[256,256]{1,0:T(8,128)S(1)}, f32[256,256]{1,0:T(8,128)}, u32[]{:S(2)}) copy-start(f32[256,256]{1,0:T(8,128)} %constant.61.clone.slope_x_ref) | copy-start | bytes 786436
  16.1 23.8 %copy-start.13 = (f32[128,128]{1,0:T(8,128)S(1)}, f32[128,128]{1,0:T(8,128)}, u32[]{:S(2)}) copy-start(f32[128,128]{1,0:T(8,128)} %constant.60.clone.slope_z_ref) | copy-start | bytes 196612
  35.2 19.8 %all-to-all-start = ((f32[640,2,128]{2,1,0:T(2,128)}), f32[640,2,128]{2,1,0:T(2,128)S(1)}, u32[]{:S(2)}, u32[]{:S(2)}) async-start(f32[640,2,128]{2,1,0:T(2,128)} %bitcast.1), calls=%async_computation | async-start | bytes 1310720 | tf_op jit(solution)/shard_map/all_to_all | solution.py:455
  55.0 24.0 %all-to-all-start.3 = ((f32[256,8,128]{2,1,0:T(8,128)}), f32[256,8,128]{2,1,0:T(8,128)S(1)}, u32[]{:S(2)}, u32[]{:S(2)}) async-start(f32[256,8,128]{2,1,0:T(8,128)} %bitcast.12), calls=%async_computation.3 | async-start | bytes 2097152 | tf_op jit(solution)/shard_map/all_to_all | solution.py:455
  65.9 1.2 %copy-start.8 = (bf16[2,2,256,512]{3,2,1,0:T(8,128)(2,1)S(1)}, bf16[2,2,256,512]{3,2,1,0:T(8,128)(2,1)}, u32[]{:S(2)}) copy-start(bf16[2,2,256,512]{3,2,1,0:T(8,128)(2,1)} %constant.64.clone.wx_ref) | copy-start | bytes 3145732
  65.9 1.5 %copy-start.9 = (bf16[2,2,512,256]{3,2,1,0:T(8,128)(2,1)S(1)}, bf16[2,2,512,256]{3,2,1,0:T(8,128)(2,1)}, u32[]{:S(2)}) copy-start(bf16[2,2,512,256]{3,2,1,0:T(8,128)(2,1)} %constant.67.clone.wxi_ref) | copy-start | bytes 3145732
  65.9 1.7 %copy-start.10 = (bf16[2,512,256]{2,1,0:T(8,128)(2,1)S(1)}, bf16[2,512,256]{2,1,0:T(8,128)(2,1)}, u32[]{:S(2)}) copy-start(bf16[2,512,256]{2,1,0:T(8,128)(2,1)} %constant.65.clone.wz_ref) | copy-start | bytes 1572868
  65.9 1.7 %copy-start.11 = (bf16[2,2,128,256]{3,2,1,0:T(8,128)(2,1)S(1)}, bf16[2,2,128,256]{3,2,1,0:T(8,128)(2,1)}, u32[]{:S(2)}) copy-start(bf16[2,2,128,256]{3,2,1,0:T(8,128)(2,1)} %constant.66.clone.wzi_ref) | copy-start | bytes 786436
  76.6 9.9 %copy-start.5 = (f32[256,256]{1,0:T(8,128)S(1)}, f32[256,256]{1,0:T(8,128)}, u32[]{:S(2)}) copy-start(f32[256,256]{1,0:T(8,128)} %constant.59.clone.slope_ref) | copy-start | bytes 786436
  79.0 24.0 %copy-start.3 = (bf16[2,256,512]{2,1,0:T(8,128)(2,1)S(1)}, bf16[2,256,512]{2,1,0:T(8,128)(2,1)}, u32[]{:S(2)}) copy-start(bf16[2,256,512]{2,1,0:T(8,128)(2,1)} %constant.68.clone.table_ref) | copy-start | bytes 1572868
  79.0 24.0 %copy-start.7 = (bf16[256,256]{1,0:T(8,128)(2,1)S(1)}, bf16[256,256]{1,0:T(8,128)(2,1)}, u32[]{:S(2)}) copy-start(bf16[256,256]{1,0:T(8,128)(2,1)} %constant.69.clone.parity_ref) | copy-start | bytes 393220
  79.0 24.0 %all-to-all-start.2 = ((f32[384,4,128]{2,1,0:T(4,128)}), f32[384,4,128]{2,1,0:T(4,128)S(1)}, u32[]{:S(2)}, u32[]{:S(2)}) async-start(f32[384,4,128]{2,1,0:T(4,128)} %bitcast.10), calls=%async_computation.2 | async-start | bytes 1572864 | tf_op jit(solution)/shard_map/all_to_all | solution.py:455
where the time goes:
time: 105 us; the launch traced here: 104 us
  waiting for transfers between devices  43.1 us (41%)
  starting transfers between devices  28.3 us (27%)
  Pallas kernels  22.2 us (21%)
  local copies, waits for them, and re-layouts  9.76 us (9%)
    all_to_all x4, waiting for transfers between devices, exchange(): out = lax.all_to_all(shaped, GZ, split_axis=0, concat_axis=0, tiled=True)  43.1 us
    all_to_all x4, starting transfers between devices, exchange(): out = lax.all_to_all(shaped, GZ, split_axis=0, concat_axis=0, tiled=True)  28.3 us
    pallas_call x1, Pallas kernels, per_device(): call(hartree_kernel, arr(ND * D_ROWS, 128), 8, 4000000000, scratch=[pltpu...  9.02 us
    pallas_call x1, Pallas kernels, per_device(): call(xc_kernel, [arr(ND * A_ROWS, 128), arr(1, 1)], 3, 4000000000, scratc...  7.55 us
    slice x1, local copies, waits for them, and re-layouts, per_device(): filt = jnp.stack([picked[:, 0], picked[:, 1], kernel_hat[:, 0]])  5.01 us
    unnamed x29, local copies, waits for them, and re-layouts  3.63 us
  transfers between devices with their start and end apart: 4, of which 4 were waited for; matrix products, arithmetic and copies ran while one was open for 6% of the time, Pallas kernels for 18%

commit v1 on v0

--- a/solution.py
+++ b/solution.py
@@ -26,19 +26,16 @@
 NZ, NY, NX = 128, 256, 256
 MZ, MY, MX = 256, 512, 512
 ND = 128
-A_ROWS = 16
-B_ROWS = 10
-D_ROWS = 12
+HART = 16
+OUT_ROWS = 26
+BACK_ROWS = 27
 CELLS = NZ * NY * NX
+Z_CHUNK = 32
+XC_ROWS = 8
+NORM = 1.0 / (MX * MY * MZ)
 VMEM = pl.BlockSpec(memory_space=pltpu.VMEM)
 SMEM = pl.BlockSpec(memory_space=pltpu.SMEM)
-
-
-def slope_matrix(n):
-    m = np.zeros((n, n))
-    for k, c in enumerate(STENCIL, 1):
-        m += np.diag(np.full(n - k, c / HGRID), k) - np.diag(np.full(n - k, c / HGRID), -k)
-    return m.astype(np.float32)
+HBM = pl.BlockSpec(memory_space=pltpu.HBM)
 
 
 def halves(m):
@@ -48,81 +45,14 @@
     return np.stack([hi, lo])
 
 
-def owned_frequencies():
-    q = np.arange(ND)
+def y_forward():
+    y, q = np.arange(NY), np.arange(ND)
     first = np.where(q < ND // 2, 4 * q + 1, 4 * q)
-    return first, first + 1
-
-
-def y_forward():
-    y = np.arange(NY)
     rows = []
-    for ky in owned_frequencies():
+    for ky in (first, first + 1):
         angle = 2.0 * np.pi * (np.outer(ky, y) % MY) / MY
         rows += [np.cos(angle), -np.sin(angle)]
     return halves(np.concatenate(rows, 0))
-
-
-def y_backward():
-    y = np.arange(NY)
-    cols = []
-    for ky in owned_frequencies():
-        angle = 2.0 * np.pi * (np.outer(y, ky) % MY) / MY
-        weight = np.where(ky == MY // 2, 1.0, 2.0) / (MX * MY * MZ)
-        cols += [np.cos(angle) * weight, -np.sin(angle) * weight]
-    return halves(np.concatenate(cols, 1))
-
-
-def parity_matrix():
-    m = np.zeros((NX, NX), np.float32)
-    x = np.arange(NX)
-    m[x, (x % 2) * (NX // 2) + x // 2] = 1.0
-    return m
-
-
-def rotation(angle):
-    c, s = np.cos(angle), np.sin(angle)
-    return np.block([[c, s], [-s, c]])
-
-
-def x_forward():
-    out = []
-    k = np.arange(MX // 2)
-    for parity in (0, 1):
-        x = 2 * np.arange(NX // 2) + parity
-        out.append(rotation(2.0 * np.pi * (np.outer(k, x) % MX) / MX).T)
-    return np.stack([halves(m) for m in out])
-
-
-def x_backward():
-    out = []
-    k = np.arange(MX // 2)
-    for parity in (0, 1):
-        x = 2 * np.arange(NX // 2) + parity
-        out.append(rotation(2.0 * np.pi * (np.outer(k, x) % MX) / MX))
-    return np.stack([halves(m) for m in out])
-
-
-Z_CHUNK = 32
-
-
-def z_forward():
-    z = np.arange(NZ)
-    rows = []
-    for c in range(0, NZ, Z_CHUNK):
-        low = np.arange(c, c + Z_CHUNK)
-        kz = np.concatenate([low, low + NZ])
-        rows.append(rotation(2.0 * np.pi * (np.outer(kz, z) % MZ) / MZ))
-    return halves(np.concatenate(rows, 0))
-
-
-def z_backward():
-    out = []
-    k = np.arange(NZ)
-    for parity in (0, 1):
-        z = 2 * np.arange(NZ // 2) + parity
-        out.append(rotation(2.0 * np.pi * (np.outer(k, z) % MZ) / MZ).T)
-    return np.stack([halves(m) for m in out])
 
 
 def split(value):
@@ -137,10 +67,6 @@
 
 def dot3(a_hi, a_lo, b_hi, b_lo):
     return dot1(a_hi, b_hi) + (dot1(a_lo, b_hi) + dot1(a_hi, b_lo))
-
-
-def dot_exact(a, b):
-    return jnp.dot(a, b, precision=lax.Precision.HIGHEST, preferred_element_type=F32)
 
 
 def put_rows(ref, row, rows, value, count=ND, scale=1):
@@ -156,27 +82,121 @@
     )
 
 
-def gradient_kernel(dens_ref, slope_ref, out_ref):
+def iota(shape, dim):
+    return lax.broadcasted_iota(jnp.int32, shape, dim)
+
+
+def slope_parts(n):
+    offset = iota((n, n), 1) - iota((n, n), 0)
+    parts = []
+    coefs = halves([c / HGRID for c in STENCIL]).astype(np.float32)
+    for part in range(2):
+        value = jnp.zeros((n, n), F32)
+        for k in range(1, 5):
+            c = float(coefs[part, k - 1])
+            value = jnp.where(offset == k, c, jnp.where(offset == -k, -c, value))
+        parts.append(value.astype(BF16))
+    return parts
+
+
+def parity_matrix(transposed):
+    x, place = iota((NX, NX), int(transposed)), iota((NX, NX), 1 - int(transposed))
+    return jnp.where(place == (x & 1) * (NX // 2) + (x >> 1), 1.0, 0.0).astype(BF16)
+
+
+def cos_sin(product):
+    turn = product.astype(jnp.int32) & 511
+    quarter = (turn + 64) >> 7
+    angle = (turn - 128 * quarter).astype(F32) * (2.0 * math.pi / 512.0)
+    sq = angle * angle
+    s = angle * (
+        1.0 + sq * (-1.0 / 6.0 + sq * (1.0 / 120.0 + sq * (-1.0 / 5040.0 + sq * (1.0 / 362880.0))))
+    )
+    c = 1.0 + sq * (-0.5 + sq * (1.0 / 24.0 + sq * (-1.0 / 720.0 + sq * (1.0 / 40320.0))))
+    odd = (quarter & 1) == 1
+    c, s = jnp.where(odd, s, c), jnp.where(odd, c, s)
+    return (
+        jnp.where(((quarter + 1) & 2) == 2, -c, c),
+        jnp.where((quarter & 2) == 2, -s, s),
+    )
+
+
+def put_parts(ref, index, rows, cols, value):
+    hi, lo = split(value)
+    ref[(*index, 0, rows, cols)] = hi
+    ref[(*index, 1, rows, cols)] = lo
+
+
+def put_rotation(ref, index, row, c, s, transposed):
+    n, m = c.shape
+    top, low = slice(row, row + n), slice(row + n, row + 2 * n)
+    put_parts(ref, index, top, slice(0, m), c)
+    put_parts(ref, index, low, slice(m, 2 * m), c)
+    put_parts(ref, index, top, slice(m, 2 * m), -s if transposed else s)
+    put_parts(ref, index, low, slice(0, m), s if transposed else -s)
+
+
+def float_iota(shape, dim):
+    return iota(shape, dim).astype(F32)
+
+
+def tables_kernel(wx_ref, wz_ref, wzi_ref, wxi_ref, yb_ref, slope_ref, slope_z_ref):
+    for parity in range(2):
+        shape = (NX // 2, MX // 2)
+        x = 2.0 * float_iota(shape, 0) + parity
+        put_rotation(wx_ref, (parity,), 0, *cos_sin(x * float_iota(shape, 1)), True)
+        shape = (MX // 2, NX // 2)
+        x = 2.0 * float_iota(shape, 1) + parity
+        put_rotation(wxi_ref, (parity,), 0, *cos_sin(x * float_iota(shape, 0)), False)
+        shape = (NZ // 2, NZ)
+        z = 4.0 * float_iota(shape, 0) + 2.0 * parity
+        put_rotation(wzi_ref, (parity,), 0, *cos_sin(z * float_iota(shape, 1)), True)
+    for chunk in range(NZ // Z_CHUNK):
+        shape = (2 * Z_CHUNK, NZ)
+        row = iota(shape, 0)
+        kz = chunk * Z_CHUNK + jnp.where(row < Z_CHUNK, row, row + NZ - Z_CHUNK)
+        angle = 2.0 * kz.astype(F32) * float_iota(shape, 1)
+        put_rotation(wz_ref, (), chunk * 4 * Z_CHUNK, *cos_sin(angle), False)
+    for slot in range(2):
+        shape = (NY, ND)
+        q = iota(shape, 1)
+        ky = 4 * q + slot + jnp.where(q < ND // 2, 1, 0)
+        c, s = cos_sin(ky.astype(F32) * float_iota(shape, 0))
+        weight = jnp.where(ky == MY // 2, NORM, 2.0 * NORM)
+        put_parts(yb_ref, (), slice(0, NY), slice(256 * slot, 256 * slot + 128), c * weight)
+        put_parts(yb_ref, (), slice(0, NY), slice(256 * slot + 128, 256 * slot + 256), -s * weight)
+    for part, value in enumerate(slope_parts(NY)):
+        slope_ref[part] = value
+    for part, value in enumerate(slope_parts(NZ)):
+        slope_z_ref[part, :, 0:NZ] = value
+        slope_z_ref[part, :, NZ : 2 * NZ] = value
+
+
+def outward_kernel(dens_hbm, table_hbm, out_ref, dens_ref, table_ref, sems):
+    dens_copy = pltpu.make_async_copy(dens_hbm, dens_ref, sems.at[0])
+    table_copy = pltpu.make_async_copy(table_hbm, table_ref, sems.at[1])
+    dens_copy.start()
+    table_copy.start()
+    slope = slope_parts(NY)
+    parity = parity_matrix(False)
+    dens_copy.wait()
     for spin in range(2):
         field = dens_ref[spin * NY : (spin + 1) * NY, :]
-        grad = dot_exact(slope_ref[...], field)
+        grad = dot3(*slope, *split(field))
         for part in range(2):
             rows = slice(part * 128, part * 128 + 128)
-            put_rows(out_ref, spin * 4 + part * 2, A_ROWS, field[rows])
-            put_rows(out_ref, 8 + spin * 4 + part * 2, A_ROWS, grad[rows])
-
-
-def y_forward_kernel(dens_ref, parity_ref, table_ref, out_ref):
+            put_rows(out_ref, spin * 4 + part * 2, OUT_ROWS, field[rows])
+            put_rows(out_ref, 8 + spin * 4 + part * 2, OUT_ROWS, grad[rows])
     hi, lo = split(dens_ref[0:NY, :] + dens_ref[NY : 2 * NY, :])
-    parity = parity_ref[...]
     hi, lo = dot1(hi, parity), dot1(lo, parity)
     mean_row = jnp.sum(hi + lo, axis=0, keepdims=True)
-    put_rows(out_ref, 8, B_ROWS, jnp.broadcast_to(mean_row, (ND, NX)))
+    put_rows(out_ref, HART + 8, OUT_ROWS, jnp.broadcast_to(mean_row, (ND, NX)))
     hi, lo = hi.astype(BF16), lo.astype(BF16)
+    table_copy.wait()
     for s in range(4):
         rows = slice(s * ND, (s + 1) * ND)
         value = dot3(table_ref[0, rows, :], table_ref[1, rows, :], hi, lo)
-        put_rows(out_ref, s * 2, B_ROWS, value)
+        put_rows(out_ref, HART + s * 2, OUT_ROWS, value)
 
 
 def pw_piece(root, params):
@@ -287,18 +307,28 @@
     )
 
 
-def xc_kernel(in_ref, slope_z_ref, slope_x_ref, out_ref, energy_ref, dens, gz, gy, gx):
+def slope_along_z(slope_z_ref, hi, lo):
+    both = jnp.concatenate([hi, lo], axis=0)
+    return dot1(slope_z_ref[0], both) + dot1(slope_z_ref[1], both)
+
+
+def slope_along_x(slope_ref, hi, lo):
+    return -dot3(hi, lo, slope_ref[0], slope_ref[1])
+
+
+def xc_part(in_ref, slope_ref, slope_z_ref, out_ref, dens, gz, gy, gx):
     for spin in range(2):
         for part in range(2):
             rows = slice(part * 128, part * 128 + 128)
-            field = get_rows(in_ref, spin * 4 + part * 2, A_ROWS)
+            field = get_rows(in_ref, spin * 4 + part * 2, OUT_ROWS)
             dens[spin, rows, :] = field
-            gy[spin, rows, :] = get_rows(in_ref, 8 + spin * 4 + part * 2, A_ROWS)
-            gz[spin, rows, :] = dot_exact(slope_z_ref[...], field)
-        gx[spin] = dot_exact(dens[spin], slope_x_ref[...])
+            gy[spin, rows, :] = get_rows(in_ref, 8 + spin * 4 + part * 2, OUT_ROWS)
+            hi, lo = split(field)
+            gz[spin, rows, :] = slope_along_z(slope_z_ref, hi, lo)
+            gx[spin, rows, :] = slope_along_x(slope_ref, hi, lo)
 
     def chunk(i, total):
-        rows = pl.ds(pl.multiple_of(i * 8, 8), 8)
+        rows = pl.ds(pl.multiple_of(i * XC_ROWS, XC_ROWS), XC_ROWS)
         zu, zd = gz[0, rows, :], gz[1, rows, :]
         yu, yd = gy[0, rows, :], gy[1, rows, :]
         xu, xd = gx[0, rows, :], gx[1, rows, :]
@@ -316,25 +346,22 @@
             ref[1, rows, :] = 2.0 * d_dd * gd + d_ud * gu
         return total + energy
 
-    total = lax.fori_loop(0, 32, chunk, jnp.zeros((8, NX), F32))
-    energy_ref[0, 0] = jnp.sum(total)
+    total = lax.fori_loop(0, 256 // XC_ROWS, chunk, jnp.zeros((XC_ROWS, NX), F32))
     for spin in range(2):
-        div_x = dot_exact(gx[spin], slope_x_ref[...])
         for part in range(2):
             rows = slice(part * 128, part * 128 + 128)
-            div_z = dot_exact(slope_z_ref[...], gz[spin, rows, :])
-            put_rows(
-                out_ref, spin * 4 + part * 2, A_ROWS, dens[spin, rows, :] - (div_z + div_x[rows])
-            )
-            put_rows(out_ref, 8 + spin * 4 + part * 2, A_ROWS, gy[spin, rows, :])
-
-
-def hartree_kernel(
-    in_ref, filt_ref, weight_ref, exc_ref, wx_ref, wz_ref, wzi_ref, wxi_ref, out_ref,
-    xp, sums, back,
+            div = slope_along_z(slope_z_ref, *split(gz[spin, rows, :]))
+            div = div + slope_along_x(slope_ref, *split(gx[spin, rows, :]))
+            put_rows(out_ref, spin * 4 + part * 2, BACK_ROWS, dens[spin, rows, :] - div)
+            put_rows(out_ref, 8 + spin * 4 + part * 2, BACK_ROWS, gy[spin, rows, :])
+    return jnp.sum(total)
+
+
+def hartree_part(
+    in_ref, filt_ref, weight_ref, wx_ref, wz_ref, wzi_ref, wxi_ref, out_ref, xp, sums, back
 ):
-    even = [in_ref[pl.ds(r, ND, stride=B_ROWS), :] for r in range(0, B_ROWS, 2)]
-    odd = [in_ref[pl.ds(r, ND, stride=B_ROWS), :] for r in range(1, B_ROWS, 2)]
+    even = [in_ref[pl.ds(r, ND, stride=OUT_ROWS), :] for r in range(HART, OUT_ROWS, 2)]
+    odd = [in_ref[pl.ds(r, ND, stride=OUT_ROWS), :] for r in range(HART + 1, OUT_ROWS, 2)]
     zero = jnp.zeros((ND, 128), F32)
     even.append(zero)
     odd.append(zero)
@@ -392,53 +419,75 @@
                 for kind in range(2 if slot < 2 else 1):
                     put_rows(
                         out_ref,
-                        parity * D_ROWS + slot * 4 + kind * 2 + sign,
-                        D_ROWS,
+                        parity * BACK_ROWS + HART + slot * 4 + kind * 2 + sign,
+                        BACK_ROWS,
                         value[parity * 64 : parity * 64 + 64, kind * 128 : kind * 128 + 128],
                         count=64,
                         scale=2,
                     )
-    put_rows(out_ref, 10, D_ROWS, jnp.full((ND, 128), exc_ref[0, 0], F32))
-    put_rows(out_ref, 11, D_ROWS, jnp.full((ND, 128), jnp.sum(energy), F32))
-
-
-def divergence_kernel(in_ref, slope_ref, out_ref):
+    return jnp.sum(energy)
+
+
+def middle_kernel(
+    first_ref, weight_ref, in_ref, slope_ref, slope_z_ref, filt_hbm, wx_hbm, wz_hbm, wzi_hbm, wxi_hbm,
+    out_ref, filt_ref, wx_ref, wz_ref, wzi_ref, wxi_ref, dens, gz, gy, gx, xp, sums, back, sems,
+):
+    first = first_ref[0]
+    moves = [
+        (filt_hbm.at[:, place, :], filt_ref.at[slot])
+        for slot, place in enumerate((first, first + 1, 0))
+    ]
+    moves += [(wx_hbm, wx_ref), (wz_hbm, wz_ref), (wzi_hbm, wzi_ref), (wxi_hbm, wxi_ref)]
+    copies = [
+        pltpu.make_async_copy(source, target, sems.at[i]) for i, (source, target) in enumerate(moves)
+    ]
+    for copy in copies:
+        copy.start()
+    exc = xc_part(in_ref, slope_ref, slope_z_ref, out_ref, dens, gz, gy, gx)
+    for copy in copies:
+        copy.wait()
+    power = hartree_part(
+        in_ref, filt_ref, weight_ref, wx_ref, wz_ref, wzi_ref, wxi_ref, out_ref, xp, sums, back
+    )
+    energies = jnp.where(iota((ND, 128), 1) < 64, exc, power)
+    put_rows(out_ref, BACK_ROWS - 1, BACK_ROWS, energies)
+
+
+def homeward_kernel(in_ref, yb_ref, slope_ref, out_ref, energy_ref):
+    field = jnp.concatenate(
+        [get_rows(in_ref, HART + 2 * s, BACK_ROWS) for s in range(4)], axis=0
+    )
+    grid = dot3(yb_ref[0], yb_ref[1], *split(field))
+    mean_row = jnp.concatenate(
+        [in_ref[HART + 8 : HART + 9, :], in_ref[HART + 9 : HART + 10, :]], axis=1
+    )
+    grid = grid + mean_row * NORM
+    hi, lo = split(grid)
+    parity = parity_matrix(True)
+    hartree = dot1(hi, parity) + dot1(lo, parity)
     for spin in range(2):
-        flux = jnp.concatenate(
-            [get_rows(in_ref, 8 + spin * 4 + part * 2, A_ROWS) for part in range(2)], axis=0
+        flux, rest = (
+            jnp.concatenate(
+                [get_rows(in_ref, base + spin * 4 + part * 2, BACK_ROWS) for part in range(2)],
+                axis=0,
+            )
+            for base in (8, 0)
         )
-        rest = jnp.concatenate(
-            [get_rows(in_ref, spin * 4 + part * 2, A_ROWS) for part in range(2)], axis=0
-        )
-        out_ref[spin * NY : (spin + 1) * NY, :] = rest - dot_exact(slope_ref[...], flux)
-
-
-def potential_kernel(in_ref, v_ref, table_ref, parity_ref, out_ref, energy_ref):
-    field = jnp.concatenate([get_rows(in_ref, 2 * s, D_ROWS) for s in range(4)], axis=0)
-    hi, lo = split(field)
-    grid = dot3(table_ref[0], table_ref[1], hi, lo)
-    mean_row = jnp.concatenate([in_ref[8:9, :], in_ref[9:10, :]], axis=1)
-    grid = grid + mean_row * (1.0 / (MX * MY * MZ))
-    hi, lo = split(grid)
-    hartree = dot1(hi, parity_ref[...]) + dot1(lo, parity_ref[...])
-    for spin in range(2):
         rows = slice(spin * NY, (spin + 1) * NY)
-        out_ref[rows, :] = v_ref[rows, :] + hartree
-    exc = jnp.sum(in_ref[pl.ds(10, ND, stride=D_ROWS), :], axis=0, keepdims=True)
-    power = jnp.sum(in_ref[pl.ds(11, ND, stride=D_ROWS), :], axis=0, keepdims=True)
-    energy_ref[0] = jnp.sum(exc) * (1.0 / (128.0 * CELLS))
-    energy_ref[1] = jnp.sum(power) * (0.5 / (128.0 * CELLS * MX * MY * MZ))
-
-
-def call(kernel, outs, n_in, flops, scratch=(), smem_in=(), smem_out=(), limit=48):
-    single = not isinstance(outs, (list, tuple))
-    shapes = [outs] if single else list(outs)
-    specs = [SMEM if i in smem_out else VMEM for i in range(len(shapes))]
+        out_ref[rows, :] = rest + hartree - dot3(slope_ref[0], slope_ref[1], *split(flux))
+    row = jnp.sum(in_ref[pl.ds(BACK_ROWS - 1, ND, stride=BACK_ROWS), :], axis=0, keepdims=True)
+    first = iota((1, 128), 1) < 64
+    energy_ref[0] = jnp.sum(jnp.where(first, row, 0.0)) * (1.0 / (64.0 * CELLS))
+    energy_ref[1] = jnp.sum(jnp.where(first, 0.0, row)) * (0.5 * NORM / (64.0 * CELLS))
+
+
+def call(kernel, outs, in_specs, flops, scratch=(), smem_out=(), limit=40):
+    specs = [SMEM if i in smem_out else VMEM for i in range(len(outs))]
     return pl.pallas_call(
         kernel,
-        out_shape=shapes[0] if single else shapes,
-        in_specs=[SMEM if i in smem_in else VMEM for i in range(n_in)],
-        out_specs=specs[0] if single else specs,
+        out_shape=list(outs),
+        in_specs=in_specs,
+        out_specs=specs,
         scratch_shapes=list(scratch),
         cost_estimate=pl.CostEstimate(flops=flops, bytes_accessed=4 << 20, transcendentals=0),
         compiler_params=pltpu.CompilerParams(vmem_limit_bytes=limit << 20),
@@ -446,8 +495,12 @@
     )
 
 
-def arr(*shape):
-    return jax.ShapeDtypeStruct(shape, F32)
+def in_hbm(value):
+    return pltpu.with_memory_space_constraint(value, pltpu.HBM)
+
+
+def arr(*shape, dtype=F32):
+    return jax.ShapeDtypeStruct(shape, dtype)
 
 
 def exchange(value, rows, group):
@@ -458,21 +511,31 @@
 
 def per_device(density, kernel_hat):
     q = lax.axis_index(GZ)
-    dens = density.reshape(2 * NY, NX)
-    slope_y = jnp.asarray(slope_matrix(NY))
-    slope_z = jnp.asarray(slope_matrix(NZ))
-    slope_x = jnp.asarray(slope_matrix(NX).T.copy())
-    parity = parity_matrix()
-
-    a_out = call(gradient_kernel, arr(ND * A_ROWS, 128), 2, 400_000_000)(dens, slope_y)
-    a_in = exchange(a_out, A_ROWS, 8)
-    b_out = call(y_forward_kernel, arr(ND * B_ROWS, 128), 3, 300_000_000)(
-        dens, jnp.asarray(parity.astype(BF16)), jnp.asarray(y_forward())
-    )
-    b_in = exchange(b_out, B_ROWS, 2)
-    start = jnp.where(q < ND // 2, 1, 0)
-    picked = lax.dynamic_slice_in_dim(kernel_hat, start, 2, axis=1)
-    filt = jnp.stack([picked[:, 0], picked[:, 1], kernel_hat[:, 0]])
+    (outward,) = call(
+        outward_kernel,
+        [arr(ND * OUT_ROWS, 128)],
+        [HBM, HBM],
+        400_000_000,
+        scratch=[
+            pltpu.VMEM((2 * NY, NX), F32),
+            pltpu.VMEM((2, 4 * ND, NY), BF16),
+            pltpu.SemaphoreType.DMA((2,)),
+        ],
+    )(in_hbm(density.reshape(2 * NY, NX)), in_hbm(jnp.asarray(y_forward())))
+    arrived = exchange(outward, OUT_ROWS, 2)
+    shapes = [(2, 2, NX, MX), (2, 2 * MZ, 2 * NZ), (2, 2, NZ, 2 * NZ), (2, 2, MX, NX)]
+    wx, wz, wzi, wxi, yb, slope, slope_z = call(
+        tables_kernel,
+        [arr(*shape, dtype=BF16) for shape in shapes]
+        + [
+            arr(2, NY, 4 * ND, dtype=BF16),
+            arr(2, NY, NY, dtype=BF16),
+            arr(2, NZ, 2 * NZ, dtype=BF16),
+        ],
+        [],
+        2_000_000_000,
+    )()
+    start = jnp.where(q < ND // 2, 1, 0).astype(jnp.int32).reshape(1)
     weights = jnp.stack(
         [
             jnp.where(q == ND // 2, 1.0, 2.0),
@@ -480,42 +543,30 @@
             jnp.where(q == 0, 1.0, 0.0),
         ]
     ).astype(F32)
-    field = pltpu.VMEM((2, NY, NX), F32)
-    c_out, exc = call(
-        xc_kernel,
-        [arr(ND * A_ROWS, 128), arr(1, 1)],
-        3,
-        4_000_000_000,
-        scratch=[field] * 4,
-        smem_out=(1,),
-    )(a_in, slope_z, slope_x)
-    c_in = exchange(c_out, A_ROWS, 8)
-    d_out = call(
-        hartree_kernel,
-        arr(ND * D_ROWS, 128),
-        8,
-        4_000_000_000,
-        scratch=[
+    field = pltpu.VMEM((2, 256, NX), F32)
+    (back,) = call(
+        middle_kernel,
+        [arr(ND * BACK_ROWS, 128)],
+        [SMEM, SMEM] + [VMEM] * 3 + [HBM] * 5,
+        8_000_000_000,
+        scratch=[pltpu.VMEM((3, MZ, MX), F32)]
+        + [pltpu.VMEM(shape, BF16) for shape in shapes]
+        + [field] * 4
+        + [
             pltpu.VMEM((3, 2, 256, 512), BF16),
             pltpu.VMEM((2, 2, 256, 512), BF16),
             pltpu.VMEM((2, 2, 128, 512), BF16),
+            pltpu.SemaphoreType.DMA((7,)),
         ],
-        smem_in=(2, 3),
-    )(
-        b_in,
-        filt,
-        weights,
-        exc,
-        jnp.asarray(x_forward()),
-        jnp.asarray(z_forward()),
-        jnp.asarray(z_backward()),
-        jnp.asarray(x_backward()),
-    )
-    d_in = exchange(d_out, D_ROWS, 4)
-    v = call(divergence_kernel, arr(2 * NY, NX), 2, 500_000_000)(c_in, slope_y)
+    )(start, weights, arrived, slope, slope_z, *map(in_hbm, (kernel_hat, wx, wz, wzi, wxi)))
+    returned = exchange(back, BACK_ROWS, 1)
     potential, energies = call(
-        potential_kernel, [arr(2 * NY, NX), arr(2)], 4, 500_000_000, smem_out=(1,)
-    )(d_in, v, jnp.asarray(y_backward()), jnp.asarray(parity.T.astype(BF16)))
+        homeward_kernel,
+        [arr(2 * NY, NX), arr(2)],
+        [VMEM] * 3,
+        1_000_000_000,
+        smem_out=(1,),
+    )(returned, yb, slope)
     return potential.reshape(2, 1, NY, NX), energies
 
 

time: 105 us -> 87.3 us (0.83)
  blocking collectives: 0 us -> 31.1 us
  waiting for transfers between devices: 43.1 us -> 20.7 us
  starting transfers between devices: 28.3 us -> 11.5 us
  local copies, waits for them, and re-layouts: 9.76 us -> 3.45 us
  Pallas kernels: 22.2 us -> 19.6 us
    all_to_all x0 -> x1, blocking collectives: none -> 31.1 us  [exchange(): out = lax.all_to_all(shaped, GZ, split_axis=0, concat_axis=0, tiled=True)]
    all_to_all x4 -> x1, waiting for transfers between devices: 43.1 us -> 20.7 us  [exchange(): out = lax.all_to_all(shaped, GZ, split_axis=0, concat_axis=0, tiled=True)]
    all_to_all x4 -> x1, starting transfers between devices: 28.3 us -> 11.5 us  [exchange(): out = lax.all_to_all(shaped, GZ, split_axis=0, concat_axis=0, tiled=True)]
    slice x1 -> x0, local copies, waits for them, and re-layouts: 5.01 us -> none  [per_device(): filt = jnp.stack([picked[:, 0], picked[:, 1], kernel_hat[:, 0]])]
    pallas_call x6 -> x4, Pallas kernels: 22.2 us -> 19.6 us  [the longest x1 12.6 us: per_device(): call(middle_kernel, [arr(ND * BACK_ROWS, 128)], [SMEM, SMEM] + [VMEM] * 3...]
    another operation x1 -> x0, local copies, waits for them, and re-layouts: 1.11 us -> none  [per_device(): filt = jnp.stack([picked[:, 0], picked[:, 1], kernel_hat[:, 0]])]
    unnamed x29 -> x8, local copies, waits for them, and re-layouts: 3.63 us -> 3.45 us
  transfers between devices with their start and end apart: 4 -> 1, of which waited for: 4 -> 1; matrix products, arithmetic and copies ran while one was open for 6% -> 0% of each run, Pallas kernels for 18% -> 2%
where the time goes in v1:
time: 87.3 us; the launch traced here: 87.1 us
  blocking collectives  31.1 us (36%)
  waiting for transfers between devices  20.7 us (24%)
  Pallas kernels  19.6 us (22%)
  starting transfers between devices  11.5 us (13%)
  local copies, waits for them, and re-layouts  3.45 us (4%)
    all_to_all x1, blocking collectives, exchange(): out = lax.all_to_all(shaped, GZ, split_axis=0, concat_axis=0, tiled=True)  31.1 us
    all_to_all x1, waiting for transfers between devices, exchange(): out = lax.all_to_all(shaped, GZ, split_axis=0, concat_axis=0, tiled=True)  20.7 us
    pallas_call x1, Pallas kernels, per_device(): call(middle_kernel, [arr(ND * BACK_ROWS, 128)], [SMEM, SMEM] + [VMEM] * 3...  12.6 us
    all_to_all x1, starting transfers between devices, exchange(): out = lax.all_to_all(shaped, GZ, split_axis=0, concat_axis=0, tiled=True)  11.5 us
    unnamed x8, local copies, waits for them, and re-layouts  3.45 us
    pallas_call x1, Pallas kernels, per_device(): call(outward_kernel, [arr(ND * OUT_ROWS, 128)], [HBM, HBM], 400000000, sc...  3.15 us
    pallas_call x1, Pallas kernels, per_device(): call(tables_kernel, [arr(*shape, dtype=BF16) for shape in shapes] + [arr(...  1.96 us
    pallas_call x1, Pallas kernels, per_device(): call(homeward_kernel, [arr(2 * NY, NX), arr(2)], [VMEM] * 3, 1000000000,...  1.92 us
  transfers between devices with their start and end apart: 1, of which 1 were waited for; matrix products, arithmetic and copies ran while one was open for 0% of the time, Pallas kernels for 2%

profile of v1, /device:TPU:1, one launch (start us, length us, event | category | flops | bytes accessed | tf_op | source)
XLA Modules:
  0.0 87.1 jit_solution(2492412145885107884)
XLA Ops:
  0.6 3.2 %outward_kernel.1 = f32[3328,128]{1,0:T(8,128)} custom-call(f32[512,256]{1,0:T(8,128)} %bitcast.16, bf16[2,512,256]{2,1,0:T(8,128)(2,1)} %constant.37.clone.table_hbm), custom_call_target="tpu_custom_call" | custom-call | flops 400000000 | bytes 4194304 | tf_op jit(solution)/shard_map/outward_kernel/pallas_call | solution.py:514
  3.8 11.5 %all-to-all-start = ((f32[1664,2,128]{2,1,0:T(2,128)}), f32[1664,2,128]{2,1,0:T(2,128)S(1)}, u32[]{:S(2)}, u32[]{:S(2)}) async-start(f32[1664,2,128]{2,1,0:T(2,128)} %bitcast.4), calls=%async_computation | async-start | bytes 3407872 | tf_op jit(solution)/shard_map/all_to_all | solution.py:508
  15.3 0.1 pad_maximum_fusion.weight_ref
  15.4 2.0 %tables_kernel.1 = (bf16[2,2,256,512]{3,2,1,0:T(8,128)(2,1)S(1)}, bf16[2,512,256]{2,1,0:T(8,128)(2,1)S(1)}, bf16[2,2,128,256]{3,2,1,0:T(8,128)(2,1)S(1)}, bf16[2...) custom-call(), custom_call_target="tpu_custom_call" | custom-call | flops 2000000000 | bytes 4194304 | tf_op jit(solution)/shard_map/tables_kernel/pallas_call | solution.py:527
  17.4 0.0 copy-start
  17.4 1.0 %copy-done = bf16[2,2,256,512]{3,2,1,0:T(8,128)(2,1)} copy-done((bf16[2,2,256,512]{3,2,1,0:T(8,128)(2,1)}, bf16[2,2,256,512]{3,2,1,0:T(8,128)(2,1)S(1)}, u32[]{:S(2)}) %copy-start) | copy-done | bytes 1048600
  18.4 0.0 copy-start.1
  18.4 1.0 %copy-done.1 = bf16[2,2,512,256]{3,2,1,0:T(8,128)(2,1)} copy-done((bf16[2,2,512,256]{3,2,1,0:T(8,128)(2,1)}, bf16[2,2,512,256]{3,2,1,0:T(8,128)(2,1)S(1)}, u32[]{:S(2)}) %copy-start.1) | copy-done | bytes 1048600
  19.3 0.0 copy-start.2
  19.3 0.8 copy-done.2
  20.1 0.0 copy-start.3
  20.1 0.7 copy-done.3
  20.8 20.7 %all-to-all-done = f32[1664,2,128]{2,1,0:T(2,128)S(1)} async-done(((f32[1664,2,128]{2,1,0:T(2,128)}), f32[1664,2,128]{2,1,0:T(2,128)S(1)}, u32[]{:S(2)}, u32[]{:S(2)}) %all-to-all-start) | async-done | bytes 1703968 | tf_op jit(solution)/shard_map/all_to_all | solution.py:508
  41.5 12.6 %middle_kernel.1 = f32[3456,128]{1,0:T(8,128)S(1)} custom-call(s32[1]{0:T(128)} %bitcast.first_ref, f32[3]{0:T(128)S(1)} %pad_maximum_fusion.weight_ref, f32[3328,128]{1,0:T(8,128)S(1)} %bitcast.15, bf16[2,256,256]{2,1,0:T(8,128)(2,1)S(1)} %get-tuple-element.11.slope_ref, bf16[2,128,256]{2,1,0:T(8,128)(2,1)S(1)} %get-tuple-element.12.slope_z_ref, ...), custom_call_target="tpu_custom_call" | custom-call | flops 8000000000 | bytes 4194304 | tf_op jit(solution)/shard_map/middle_kernel/pallas_call | solution.py:547
  54.1 31.1 %all_to_all.10 = f32[3456,1,128]{2,1,0:T(1,128)S(1)} all-to-all(f32[3456,1,128]{2,1,0:T(1,128)S(1)} %bitcast.13), channel_id=1, replica_groups=mesh['gz_0'=4,'gz_1'=4,'gz_2'=4,'gz_3'=2] {'gz_0','gz_1','gz_2','gz_3'}, dimensions={0} | all-to-all | bytes 3538944 | tf_op jit(solution)/shard_map/all_to_all | solution.py:508
  85.2 1.9 %homeward_kernel.1 = (f32[512,256]{1,0:T(8,128)}, f32[2]{0:T(128)}) custom-call(f32[3456,128]{1,0:T(8,128)S(1)} %bitcast.14, bf16[2,256,512]{2,1,0:T(8,128)(2,1)S(1)} %get-tuple-element.17.yb_ref, bf16[2,256,256]{2,1,0:T(8,128)(2,1)S(1)} %get-tuple-element.11.slope_ref), custom_call_target="tpu_custom_call" | custom-call | flops 1000000000 | bytes 4194304 | tf_op jit(solution)/shard_map/homeward_kernel/pallas_call | solution.py:563
Async XLA Ops:
  3.8 37.7 %all-to-all-start = ((f32[1664,2,128]{2,1,0:T(2,128)}), f32[1664,2,128]{2,1,0:T(2,128)S(1)}, u32[]{:S(2)}, u32[]{:S(2)}) async-start(f32[1664,2,128]{2,1,0:T(2,128)} %bitcast.4), calls=%async_computation | async-start | bytes 3407872 | tf_op jit(solution)/shard_map/all_to_all | solution.py:508
  17.4 1.0 %copy-start = (bf16[2,2,256,512]{3,2,1,0:T(8,128)(2,1)}, bf16[2,2,256,512]{3,2,1,0:T(8,128)(2,1)S(1)}, u32[]{:S(2)}) copy-start(bf16[2,2,256,512]{3,2,1,0:T(8,128)(2,1)S(1)} %get-tuple-element.13.wx_hbm) | copy-start | bytes 3145732
  18.4 1.0 %copy-start.1 = (bf16[2,2,512,256]{3,2,1,0:T(8,128)(2,1)}, bf16[2,2,512,256]{3,2,1,0:T(8,128)(2,1)S(1)}, u32[]{:S(2)}) copy-start(bf16[2,2,512,256]{3,2,1,0:T(8,128)(2,1)S(1)} %get-tuple-element.16.wxi_hbm) | copy-start | bytes 3145732
  19.3 0.8 copy-start.2
  20.1 0.7 copy-start.3
